TPU v7x, 512 devices: a whole 4x4x16 slice. The times are simulated.
512 devices in a mesh: grad: 64 (over y_lo, z, core), flow: 8 (over x, y_hi).
Axes of the slice: x: 4, y: 4 (y_hi: 2, y_lo: 2; y = y_hi * 2 + y_lo), z: 16, core: 2. Of those that a mesh axis runs over, the one named last changes fastest.
Arguments:
- bead_pos: float32 [3, 64, 32768], P(None, 'grad', 'flow'), may hold values from 0 to 11, as said below
- bead_vel: float32 [3, 64, 32768], P(None, 'grad', 'flow'), may hold values from -5 to 5
- noise_angle: float32 [2, 64, 32768], P(None, 'grad', 'flow'), may hold values from -3.140625 to 3.140625
- occupancy: int32 [64, 512], P('grad', 'flow'), may hold values from 32 to 64
- image_shift: int32 [1], replicated, may hold values from 0 to 511
- strain: float32 [1], replicated, may hold values from 0.38 to 0.48
Outputs:
- new_pos: float32 [3, 64, 32768], P(None, 'grad', 'flow')
- new_vel: float32 [3, 64, 32768], P(None, 'grad', 'flow')
- stress_profile: float32 [64], P('grad')
Inputs may be any that keep to these rules, and one draw needn't show every extreme that they name: `bead_pos`: the first coordinate lies in [0, 2), the second in [0, 1), the third in [0, 64 / 6).
All inputs are finite; a program needn't handle non-finite values.
Results may differ from a plain program's by a relative error of at most 0.0003.
Values sent between devices are 32-bit elements; how exact they have to be, the bound alone decides.
A program may use at most 64 MiB of HBM per device.

v0:
```python
import math

import jax
import jax.numpy as jnp
from jax import lax
from jax.sharding import PartitionSpec as P

TB = 64


repulsion = 25.0
friction = 4.5
noise_gain = 15.0
time_step = 0.04
shear_rate = 0.25
root_two = 1.4142135623730951


def in_order(tiles, dim):
    dims = list(tiles.shape[1:])
    dims[dim] *= tiles.shape[0]
    return jnp.moveaxis(tiles, 0, dim).reshape(dims)


def sent_to_all(x, axis):
    copies = jnp.broadcast_to(x, (lax.axis_size(axis), *x.shape))
    return lax.all_to_all(copies, axis, split_axis=0, concat_axis=0, tiled=True)


def collect(x, axis, dim):
    return in_order(sent_to_all(x, axis), dim)


def with_halo(block, sides, width):
    for axis, dim in sides:
        count = lax.axis_size(axis)
        forward = [(i, i + 1) for i in range(count - 1)]
        forward.append((count - 1, 0))
        backward = [(target, source) for source, target in forward]
        low = lax.ppermute(
            lax.slice_in_dim(block, block.shape[dim] - width, None, axis=dim), axis, forward
        )
        high = lax.ppermute(lax.slice_in_dim(block, 0, width, axis=dim), axis, backward)
        block = jnp.concatenate([low, block, high], axis=dim)
    return block


def from_behind(x, axis, by):
    devices = lax.axis_size(axis)
    return lax.ppermute(x, axis, [(i, (i + by) % devices) for i in range(devices)])


def taken_together(x, axis):
    return sent_to_all(x, axis).sum(axis=0)


def live_slots(occupancy):
    rows_here = occupancy.shape[0]
    width = occupancy.shape[1] * TB
    slot_index = lax.broadcasted_iota(jnp.int32, (rows_here, width), 1) % TB
    limits = jnp.repeat(occupancy, TB, axis=1)
    return (slot_index < limits).astype(jnp.float32)


def band_forces(slab_band, strain_now):
    all_tiles = slab_band.shape[2] // TB
    centre_tiles = all_tiles - 2
    block_tiles = math.gcd(32, centre_tiles)
    tile_grid = slab_band.reshape(slab_band.shape[0], 3, all_tiles, TB)
    box_depth = TB / 6.0
    slot_row = lax.broadcasted_iota(jnp.int32, (TB, 3 * TB), 0)
    slot_col = lax.broadcasted_iota(jnp.int32, (TB, 3 * TB), 1)
    itself = (slot_col == slot_row + TB).astype(jnp.float32)
    offset = jnp.repeat(jnp.array([2.0, 0.0, -2.0], jnp.float32), TB)

    def one_block(first_tile):
        centre = lax.dynamic_slice_in_dim(tile_grid[:, 1], first_tile + 1, block_tiles, 1)[
            :, :, :, None
        ]
        forces = jnp.zeros((3, block_tiles, TB), jnp.float32)
        virial = jnp.zeros((), jnp.float32)
        for band_row in range(3):
            nearby = lax.dynamic_slice_in_dim(
                tile_grid[:, band_row], first_tile, block_tiles + 2, 1
            )
            partners = jnp.concatenate(
                [nearby[:, column : column + block_tiles] for column in range(3)], 2
            )[:, :, None, :]
            sep_x = centre[0] - partners[0] + offset
            sep_y = centre[1] - partners[1] + (1.0 - band_row)
            sep_z = centre[2] - partners[2]
            sep_z = jnp.where(sep_z > 0.5 * box_depth, sep_z - box_depth, sep_z)
            sep_z = jnp.where(sep_z < -0.5 * box_depth, sep_z + box_depth, sep_z)
            phys_x = sep_x + strain_now * sep_y
            paired = centre[7] * partners[7]
            if band_row == 1:
                paired = paired * (1.0 - itself)
            weight = (
                jnp.maximum(1.0 - phys_x * phys_x - sep_y * sep_y - sep_z * sep_z, 0.0) * paired
            )
            approach = (
                phys_x * (centre[3] - partners[3])
                + sep_y * (centre[4] - partners[4])
                + sep_z * (centre[5] - partners[5])
            )
            random_kick = root_two * jnp.cos(centre[6] - partners[6])
            magnitude = weight * (
                repulsion + noise_gain * random_kick - friction * weight * approach
            )
            forces = forces + jnp.stack(
                [
                    jnp.sum(magnitude * phys_x, -1),
                    jnp.sum(magnitude * sep_y, -1),
                    jnp.sum(magnitude * sep_z, -1),
                ]
            )
            virial = virial + 0.5 * jnp.sum(magnitude * phys_x * sep_y)
        return (forces, virial)

    starts = jnp.arange(0, centre_tiles, block_tiles, dtype=jnp.int32)
    block_forces, block_virials = lax.map(one_block, starts)
    forces = jnp.transpose(block_forces, (1, 0, 2, 3)).reshape(3, centre_tiles * TB)
    return (forces, jnp.sum(block_virials))


def advance(positions, velocity, forces, strain_now):
    vel_x = velocity[0] + time_step * (forces[0] - shear_rate * velocity[1])
    vel_y = velocity[1] + time_step * forces[1]
    vel_z = velocity[2] + time_step * forces[2]
    pos_x = positions[0] + time_step * (vel_x - strain_now * vel_y)
    pos_y = positions[1] + time_step * vel_y
    pos_z = positions[2] + time_step * vel_z
    return (
        jnp.stack([pos_x, pos_y, pos_z]),
        jnp.stack([vel_x, vel_y, vel_z]),
        strain_now + shear_rate * time_step,
    )


def turn_tiles(fields, amounts):
    flow_count = lax.axis_size("flow")
    local_tiles = fields.shape[2] // TB
    total_tiles = local_tiles * flow_count
    width = local_tiles * TB
    wrapped = amounts % total_tiles
    gathered = collect(fields, "flow", 2)
    doubled = jnp.concatenate([gathered, gathered], 2)
    begins = (lax.axis_index("flow") * local_tiles + wrapped) % total_tiles * TB
    return jax.vmap(
        lambda segment, begin_at: lax.dynamic_slice_in_dim(segment, begin_at, width, 1),
        in_axes=(1, 0),
        out_axes=1,
    )(doubled, begins)


def per_device(bead_pos, bead_vel, noise_angle, occupancy, image_shift, strain):
    live_mask = live_slots(occupancy)
    grad_index = lax.axis_index("grad")
    grad_count = lax.axis_size("grad")
    image_tiles = image_shift[0]
    strain_now = strain[0]
    positions, velocity = (bead_pos, bead_vel)
    running = jnp.zeros((), jnp.float32)
    for step_index in range(2):
        fields = jnp.concatenate(
            [positions, velocity, noise_angle[step_index][None], live_mask[None]], 0
        )
        turn_by = jnp.where(
            grad_index == grad_count - 1, image_tiles, jnp.where(grad_index == 0, -image_tiles, 0)
        )
        turned = turn_tiles(fields, jnp.reshape(turn_by, (1,)))
        outgoing = jnp.stack([fields, turned])
        padded = with_halo(outgoing, (("grad", 2),), 1)
        below_row = jnp.where(grad_index == 0, padded[1, :, 0], padded[0, :, 0])
        above_row = jnp.where(grad_index == grad_count - 1, padded[1, :, 2], padded[0, :, 2])
        slab_band = jnp.stack([below_row, fields[:, 0], above_row], 1)
        slab_band = with_halo(slab_band, (("flow", 2),), TB)
        forces, virial = band_forces(slab_band, strain_now)
        kinetic = jnp.sum(live_mask * velocity[0] * velocity[1])
        running = running + kinetic + virial
        positions, velocity, strain_now = advance(positions, velocity, forces[:, None], strain_now)
    parity = (grad_index % 2).astype(jnp.float32)
    shifted_x = positions[0] + parity + positions[1]
    stacked = jnp.concatenate([shifted_x[None], positions[1:], velocity], 0)
    row_width = stacked.shape[2]
    tail_tiles = grad_count // 2
    trailing = stacked[:, :, row_width - tail_tiles * TB :]
    received = from_behind(trailing, "flow", 1)
    combined = jnp.concatenate([received, stacked], 2)
    begin_at = (tail_tiles - grad_index // 2) * TB
    remapped = lax.dynamic_slice_in_dim(combined, begin_at, row_width, 2)
    summed = taken_together(jnp.reshape(running, (1,)), "flow")
    total_tiles = bead_pos.shape[2] // TB * lax.axis_size("flow")
    box_depth = TB / 6.0
    stress_profile = -summed / (2.0 * total_tiles * 2.0 * box_depth)
    return (remapped[:3], remapped[3:], stress_profile)


def solution(mesh):
    in_specs = (
        P(None, "grad", "flow"),
        P(None, "grad", "flow"),
        P(None, "grad", "flow"),
        P("grad", "flow"),
        P(),
        P(),
    )
    out_specs = (P(None, "grad", "flow"), P(None, "grad", "flow"), P("grad"))
    return jax.shard_map(
        per_device, mesh=mesh, in_specs=in_specs, out_specs=out_specs, check_vma=False
    )
```

profile of v0, /device:TPU:8, one launch (start us, length us, event | category | flops | bytes accessed | tf_op | source)
XLA Modules:
  0.0 302.6 jit_solution(10972553230158383662)
XLA Ops:
  0.6 0.7 broadcast_in_dim.59
  1.5 0.7 slice.812
  2.2 0.9 pad_maximum_fusion.10
  3.2 1.1 broadcast_in_dim.61
  4.3 6.2 %all-to-all-start = ((f32[8,8,1,4096]{3,1,2,0:T(8,128)}), f32[8,8,1,4096]{3,1,2,0:T(8,128)S(1)}, u32[]{:S(2)}, u32[]{:S(2)}) async-start(f32[8,8,1,4096]{3,1,2,0:T(8,128)} %broadcast_in_dim.61), calls=%async_computation | async-start | bytes 2097152 | tf_op jit(solution)/shard_map/all_to_all | solution.py:27
  11.3 15.1 %all-to-all-done = f32[8,8,1,4096]{3,1,2,0:T(8,128)S(1)} async-done(((f32[8,8,1,4096]{3,1,2,0:T(8,128)}), f32[8,8,1,4096]{3,1,2,0:T(8,128)S(1)}, u32[]{:S(2)}, u32[]{:S(2)}) %all-to-all-start) | async-done | bytes 1048608 | tf_op jit(solution)/shard_map/all_to_all | solution.py:27
  26.4 0.2 fusion.45
  26.6 0.3 pad_maximum_fusion.8
  26.9 1.9 collective-permute-start
  28.8 11.0 %collective-permute-start.1 = (f32[2,8,1,4096]{3,2,1,0:T(1,128)S(1)}, f32[2,8,1,4096]{3,2,1,0:T(1,128)S(1)}, u32[]{:S(2)}, u32[]{:S(2)}) collective-permute-start(f32[2,8,1,4096]{3,2,1,0:T(1,128)S(1)} %pad_maximum_fusion.8), channel_id=1, source_target_pairs={{8,0},{16,8},{24,16},{32,24},{40,32},{48,40},{56,48},{64,56},{72,6... | collective-permute-start | bytes 786440 | tf_op jit(solution)/shard_map/ppermute | solution.py:43
  39.9 2.1 collective-permute-done
  42.0 0.1 fusion.46
  42.1 1.6 collective-permute-done.1
  43.8 0.1 fusion.48
  43.9 0.4 pad_maximum_fusion.6
  44.4 3.0 collective-permute-start.2
  47.4 6.5 %collective-permute-start.3 = (f32[8,3,64]{2,1,0:T(4,128)S(1)}, f32[8,3,64]{2,1,0:T(4,128)S(1)}, u32[]{:S(2)}, u32[]{:S(2)}) collective-permute-start(f32[8,3,64]{2,1,0:T(4,128)S(1)} %get-tuple-element.608), channel_id=1, source_target_pairs={{1,0},{2,1},{3,2},{4,3},{5,4},{6,5},{7,6},{0,7},{9,8},{10,9},{11,1... | collective-permute-start | bytes 18440 | tf_op jit(solution)/shard_map/ppermute | solution.py:43
  54.5 0.7 collective-permute-done.3
  55.2 0.7 concatenate.144
  55.9 0.4 reshape.1159
  56.4 89.9 %while.36 = (s32[]{:T(128)}, f32[2,3,32,64]{3,2,1,0:T(8,128)S(1)}, f32[2]{0:T(128)S(1)}, f32[8,3,66,64]{3,2,1,0:T(8,128)S(1)}, s32[2]{0:T(128)S(1)}, /*index=5*/...) while((s32[]{:T(128)}, f32[2,3,32,64]{3,2,1,0:T(8,128)S(1)}, ...), condition=%wide.region_13.14_spmd.clone.clone, body=%wide.region_0.13_spmd.sunk.clone.clone.sunk | while | flops 53446672 | bytes 6059237 | solution.py:121
  56.4 0.7 dynamic_slice.125
  59.3 0.1 pad_maximum_fusion.18
  61.2 12.3 %fusion.81 = (f32[]{:T(128)}, f32[32,64]{1,0:T(8,128)S(1)}, f32[32,64]{1,0:T(8,128)S(1)}, f32[32,64]{1,0:T(8,128)S(1)}) fusion(f32[32,192]{1,0:T(8,128)S(1)} %get-tuple-element.845, f32[32,192]{1,0:T(8,128)S(1)} %get-tuple-element.846, f32[32,64]{1,0:T(8,128)S(1)} %get-tuple-element.822, f32[]{:T(128)} %get-tuple-element.984, f32[192]{0:T(256)S(1)} %add.1813, ...), kind=kLoop, calls=%fused_computation.24.clone.1 | loop fusion | flops 17688576 | bytes 336648 | tf_op jit(solution)/shard_map/while/body/eval_jaxpr/reduce_sum | solution.py:117
  73.5 0.1 pad_maximum_fusion.17
  73.7 12.7 %multiply_reduce_fusion.19 = (f32[]{:T(128)}, f32[32,64]{1,0:T(8,128)S(1)}, f32[32,64]{1,0:T(8,128)S(1)}, f32[32,64]{1,0:T(8,128)S(1)}) fusion(f32[32,192]{1,0:T(8,128)S(1)} %get-tuple-element.820, f32[32,64]{1,0:T(8,128)S(1)} %get-tuple-element.822, f32[]{:T(128)} %get-tuple-element.984, f32[192]{0:T(256)S(1)} %add.1813, ...), kind=kLoop, calls=%fused_computation.26.clone.1 | loop fusion | flops 17688576 | bytes 287496 | tf_op jit(solution)/shard_map/while/body/eval_jaxpr/reduce_sum | solution.py:117
  87.8 12.7 %multiply_reduce_fusion.20 = (f32[]{:T(128)}, f32[32,64]{1,0:T(8,128)S(1)}, f32[32,64]{1,0:T(8,128)S(1)}, f32[32,64]{1,0:T(8,128)S(1)}) fusion(f32[32,192]{1,0:T(8,128)S(1)} %get-tuple-element.860, f32[32,192]{1,0:T(8,128)S(1)} %get-tuple-element.861, f32[32,64]{1,0:T(8,128)S(1)} %get-tuple-element.822, f32[]{:T(128)} %get-tuple-element.984, ...), kind=kLoop, calls=%fused_computation.25.clone.1 | loop fusion | flops 17688576 | bytes 287496 | tf_op jit(solution)/shard_map/while/body/eval_jaxpr/reduce_sum | solution.py:117
  101.4 0.7 dynamic_slice.125
  104.3 0.1 pad_maximum_fusion.18
  106.1 12.3 %fusion.81 = (f32[]{:T(128)}, f32[32,64]{1,0:T(8,128)S(1)}, f32[32,64]{1,0:T(8,128)S(1)}, f32[32,64]{1,0:T(8,128)S(1)}) fusion(f32[32,192]{1,0:T(8,128)S(1)} %get-tuple-element.845, f32[32,192]{1,0:T(8,128)S(1)} %get-tuple-element.846, f32[32,64]{1,0:T(8,128)S(1)} %get-tuple-element.822, f32[]{:T(128)} %get-tuple-element.984, f32[192]{0:T(256)S(1)} %add.1813, ...), kind=kLoop, calls=%fused_computation.24.clone.1 | loop fusion | flops 17688576 | bytes 336648 | tf_op jit(solution)/shard_map/while/body/eval_jaxpr/reduce_sum | solution.py:117
  118.5 0.1 pad_maximum_fusion.17
  118.6 12.7 %multiply_reduce_fusion.19 = (f32[]{:T(128)}, f32[32,64]{1,0:T(8,128)S(1)}, f32[32,64]{1,0:T(8,128)S(1)}, f32[32,64]{1,0:T(8,128)S(1)}) fusion(f32[32,192]{1,0:T(8,128)S(1)} %get-tuple-element.820, f32[32,64]{1,0:T(8,128)S(1)} %get-tuple-element.822, f32[]{:T(128)} %get-tuple-element.984, f32[192]{0:T(256)S(1)} %add.1813, ...), kind=kLoop, calls=%fused_computation.26.clone.1 | loop fusion | flops 17688576 | bytes 287496 | tf_op jit(solution)/shard_map/while/body/eval_jaxpr/reduce_sum | solution.py:117
  132.8 12.7 %multiply_reduce_fusion.20 = (f32[]{:T(128)}, f32[32,64]{1,0:T(8,128)S(1)}, f32[32,64]{1,0:T(8,128)S(1)}, f32[32,64]{1,0:T(8,128)S(1)}) fusion(f32[32,192]{1,0:T(8,128)S(1)} %get-tuple-element.860, f32[32,192]{1,0:T(8,128)S(1)} %get-tuple-element.861, f32[32,64]{1,0:T(8,128)S(1)} %get-tuple-element.822, f32[]{:T(128)} %get-tuple-element.984, ...), kind=kLoop, calls=%fused_computation.25.clone.1 | loop fusion | flops 17688576 | bytes 287496 | tf_op jit(solution)/shard_map/while/body/eval_jaxpr/reduce_sum | solution.py:117
  147.1 19.6 %all_to_all.16 = f32[8,8,1,4096]{3,1,2,0:T(8,128)S(1)} all-to-all(f32[8,8,1,4096]{3,1,2,0:T(8,128)S(1)} %broadcast_in_dim.64), channel_id=1, replica_groups=mesh['grad'=64,'flow'=8] {'flow'}, dimensions={0} | all-to-all | bytes 2097152 | tf_op jit(solution)/shard_map/all_to_all | solution.py:27
  166.7 0.2 fusion.44
  167.0 0.3 pad_maximum_fusion.9
  167.3 1.9 collective-permute-start.4
  169.3 7.3 %collective-permute-start.5 = (f32[2,8,1,4096]{3,2,1,0:T(1,128)S(1)}, f32[2,8,1,4096]{3,2,1,0:T(1,128)S(1)}, u32[]{:S(2)}, u32[]{:S(2)}) collective-permute-start(f32[2,8,1,4096]{3,2,1,0:T(1,128)S(1)} %pad_maximum_fusion.9), channel_id=1, source_target_pairs={{8,0},{16,8},{24,16},{32,24},{40,32},{48,40},{56,48},{64,56},{72,6... | collective-permute-start | bytes 786440 | tf_op jit(solution)/shard_map/ppermute | solution.py:43
  176.6 1.8 collective-permute-done.4
  178.6 1.7 collective-permute-done.5
  180.5 0.4 pad_maximum_fusion.7
  180.9 3.2 %collective-permute-start.6 = (f32[8,3,64]{2,1,0:T(4,128)S(1)}, f32[8,3,64]{2,1,0:T(4,128)S(1)}, u32[]{:S(2)}, u32[]{:S(2)}) collective-permute-start(f32[8,3,64]{2,1,0:T(4,128)S(1)} %get-tuple-element.607), channel_id=1, source_target_pairs={{0,1},{1,2},{2,3},{3,4},{4,5},{5,6},{6,7},{7,0},{8,9},{9,10},{10,1... | collective-permute-start | bytes 18440 | tf_op jit(solution)/shard_map/ppermute | solution.py:40
  184.1 6.2 %collective-permute-start.7 = (f32[8,3,64]{2,1,0:T(4,128)S(1)}, f32[8,3,64]{2,1,0:T(4,128)S(1)}, u32[]{:S(2)}, u32[]{:S(2)}) collective-permute-start(f32[8,3,64]{2,1,0:T(4,128)S(1)} %get-tuple-element.606), channel_id=1, source_target_pairs={{1,0},{2,1},{3,2},{4,3},{5,4},{6,5},{7,6},{0,7},{9,8},{10,9},{11,1... | collective-permute-start | bytes 18440 | tf_op jit(solution)/shard_map/ppermute | solution.py:43
  190.4 0.7 fusion.53
  191.2 0.6 collective-permute-done.7
  191.8 0.7 concatenate.148
  192.5 0.4 reshape.1160
  192.9 83.9 %while.37 = (s32[]{:T(128)}, f32[2,3,32,64]{3,2,1,0:T(8,128)S(1)}, f32[2]{0:T(128)S(1)}, f32[8,3,66,64]{3,2,1,0:T(8,128)S(1)}, s32[2]{0:T(128)S(1)}, /*index=5*/...) while((s32[]{:T(128)}, f32[2,3,32,64]{3,2,1,0:T(8,128)S(1)}, ...), condition=%wide.region_27.28_spmd.clone.clone, body=%wide.region_14.27_spmd.sunk.clone.clone.sunk | while | flops 53446672 | bytes 6059237 | solution.py:121
  193.0 0.6 dynamic_slice.128
  196.9 11.7 %fusion.87 = (f32[]{:T(128)}, f32[32,64]{1,0:T(8,128)S(1)}, f32[32,64]{1,0:T(8,128)S(1)}, f32[32,64]{1,0:T(8,128)S(1)}) fusion(f32[32,192]{1,0:T(8,128)S(1)} %get-tuple-element.910, f32[32,192]{1,0:T(8,128)S(1)} %get-tuple-element.911, f32[32,64]{1,0:T(8,128)S(1)} %get-tuple-element.887, f32[]{:T(128)} %get-tuple-element.1044, f32[192]{0:T(256)S(1)} %add.1852, ...), kind=kLoop, calls=%fused_computation.109.clone.1 | loop fusion | flops 17688576 | bytes 336648 | tf_op jit(solution)/shard_map/while/body/eval_jaxpr/reduce_sum | solution.py:117
  208.9 12.0 %multiply_reduce_fusion.21 = (f32[]{:T(128)}, f32[32,64]{1,0:T(8,128)S(1)}, f32[32,64]{1,0:T(8,128)S(1)}, f32[32,64]{1,0:T(8,128)S(1)}) fusion(f32[32,192]{1,0:T(8,128)S(1)} %get-tuple-element.885, f32[32,64]{1,0:T(8,128)S(1)} %get-tuple-element.887, f32[]{:T(128)} %get-tuple-element.1044, f32[192]{0:T(256)S(1)} %add.1852, ...), kind=kLoop, calls=%fused_computation.111.clone.1 | loop fusion | flops 17688576 | bytes 287496 | tf_op jit(solution)/shard_map/while/body/eval_jaxpr/reduce_sum | solution.py:117
  222.2 12.0 %multiply_reduce_fusion.22 = (f32[]{:T(128)}, f32[32,64]{1,0:T(8,128)S(1)}, f32[32,64]{1,0:T(8,128)S(1)}, f32[32,64]{1,0:T(8,128)S(1)}) fusion(f32[32,192]{1,0:T(8,128)S(1)} %get-tuple-element.925, f32[32,192]{1,0:T(8,128)S(1)} %get-tuple-element.926, f32[32,64]{1,0:T(8,128)S(1)} %get-tuple-element.887, f32[]{:T(128)} %get-tuple-element.1044, ...), kind=kLoop, calls=%fused_computation.110.clone.1 | loop fusion | flops 17688576 | bytes 287496 | tf_op jit(solution)/shard_map/while/body/eval_jaxpr/reduce_sum | solution.py:117
  234.9 0.6 dynamic_slice.128
  238.9 11.7 %fusion.87 = (f32[]{:T(128)}, f32[32,64]{1,0:T(8,128)S(1)}, f32[32,64]{1,0:T(8,128)S(1)}, f32[32,64]{1,0:T(8,128)S(1)}) fusion(f32[32,192]{1,0:T(8,128)S(1)} %get-tuple-element.910, f32[32,192]{1,0:T(8,128)S(1)} %get-tuple-element.911, f32[32,64]{1,0:T(8,128)S(1)} %get-tuple-element.887, f32[]{:T(128)} %get-tuple-element.1044, f32[192]{0:T(256)S(1)} %add.1852, ...), kind=kLoop, calls=%fused_computation.109.clone.1 | loop fusion | flops 17688576 | bytes 336648 | tf_op jit(solution)/shard_map/while/body/eval_jaxpr/reduce_sum | solution.py:117
  250.8 12.0 %multiply_reduce_fusion.21 = (f32[]{:T(128)}, f32[32,64]{1,0:T(8,128)S(1)}, f32[32,64]{1,0:T(8,128)S(1)}, f32[32,64]{1,0:T(8,128)S(1)}) fusion(f32[32,192]{1,0:T(8,128)S(1)} %get-tuple-element.885, f32[32,64]{1,0:T(8,128)S(1)} %get-tuple-element.887, f32[]{:T(128)} %get-tuple-element.1044, f32[192]{0:T(256)S(1)} %add.1852, ...), kind=kLoop, calls=%fused_computation.111.clone.1 | loop fusion | flops 17688576 | bytes 287496 | tf_op jit(solution)/shard_map/while/body/eval_jaxpr/reduce_sum | solution.py:117
  264.2 12.0 %multiply_reduce_fusion.22 = (f32[]{:T(128)}, f32[32,64]{1,0:T(8,128)S(1)}, f32[32,64]{1,0:T(8,128)S(1)}, f32[32,64]{1,0:T(8,128)S(1)}) fusion(f32[32,192]{1,0:T(8,128)S(1)} %get-tuple-element.925, f32[32,192]{1,0:T(8,128)S(1)} %get-tuple-element.926, f32[32,64]{1,0:T(8,128)S(1)} %get-tuple-element.887, f32[]{:T(128)} %get-tuple-element.1044, ...), kind=kLoop, calls=%fused_computation.110.clone.1 | loop fusion | flops 17688576 | bytes 287496 | tf_op jit(solution)/shard_map/while/body/eval_jaxpr/reduce_sum | solution.py:117
  277.5 4.2 %collective-permute-start.8 = (f32[6,1,2048]{2,1,0:T(1,128)S(1)}, f32[6,1,2048]{2,1,0:T(1,128)S(1)}, u32[]{:S(2)}, u32[]{:S(2)}) collective-permute-start(f32[6,1,2048]{2,1,0:T(1,128)S(1)} %slice.1218), channel_id=1, source_target_pairs={{0,1},{1,2},{2,3},{3,4},{4,5},{5,6},{6,7},{7,0},{8,9},{9,10},{10,1... | collective-permute-start | bytes 147464 | tf_op jit(solution)/shard_map/ppermute | solution.py:50
  281.7 0.7 multiply_reduce_fusion.14
  282.3 0.6 reduce_sum.358
  284.9 0.6 reduce_sum.360
  286.2 13.0 %all_to_all.17 = f32[8,1,1]{2,1,0:T(1,128)S(1)} all-to-all(f32[8,1,1]{2,1,0:T(1,128)S(1)} %broadcast_in_dim.68), channel_id=1, replica_groups=mesh['grad'=64,'flow'=8] {'flow'}, dimensions={0} | all-to-all | bytes 64 | tf_op jit(solution)/shard_map/all_to_all | solution.py:27
  299.1 0.6 reduce_sum.361
  300.4 0.4 fusion.50
  300.8 0.6 fusion.64
  (126 shorter events, 6.2 us)
Async XLA Ops:
  4.3 6.9 %copy-start = (f32[3,1,4096]{2,1,0:T(1,128)S(1)}, f32[3,1,4096]{2,1,0:T(1,128)}, u32[]{:S(2)}) copy-start(f32[3,1,4096]{2,1,0:T(1,128)} %param.12) | copy-start | bytes 147460
  4.3 6.9 %copy-start.1 = (f32[3,1,4096]{2,1,0:T(1,128)S(1)}, f32[3,1,4096]{2,1,0:T(1,128)}, u32[]{:S(2)}) copy-start(f32[3,1,4096]{2,1,0:T(1,128)} %param.13) | copy-start | bytes 147460
  4.3 22.1 %all-to-all-start = ((f32[8,8,1,4096]{3,1,2,0:T(8,128)}), f32[8,8,1,4096]{3,1,2,0:T(8,128)S(1)}, u32[]{:S(2)}, u32[]{:S(2)}) async-start(f32[8,8,1,4096]{3,1,2,0:T(8,128)} %broadcast_in_dim.61), calls=%async_computation | async-start | bytes 2097152 | tf_op jit(solution)/shard_map/all_to_all | solution.py:27
  26.9 15.1 %collective-permute-start = (f32[2,8,1,4096]{3,2,1,0:T(1,128)S(1)}, f32[2,8,1,4096]{3,2,1,0:T(1,128)S(1)}, u32[]{:S(2)}, u32[]{:S(2)}) collective-permute-start(f32[2,8,1,4096]{3,2,1,0:T(1,128)S(1)} %pad_maximum_fusion.8), channel_id=1, source_target_pairs={{0,8},{8,16},{16,24},{24,32},{32,40},{40,48},{48,56},{56,64},{64,7... | collective-permute-start | bytes 786440 | tf_op jit(solution)/shard_map/ppermute | solution.py:40
  28.8 14.9 %collective-permute-start.1 = (f32[2,8,1,4096]{3,2,1,0:T(1,128)S(1)}, f32[2,8,1,4096]{3,2,1,0:T(1,128)S(1)}, u32[]{:S(2)}, u32[]{:S(2)}) collective-permute-start(f32[2,8,1,4096]{3,2,1,0:T(1,128)S(1)} %pad_maximum_fusion.8), channel_id=1, source_target_pairs={{8,0},{16,8},{24,16},{32,24},{40,32},{48,40},{56,48},{64,56},{72,6... | collective-permute-start | bytes 786440 | tf_op jit(solution)/shard_map/ppermute | solution.py:43
  44.4 10.1 %collective-permute-start.2 = (f32[8,3,64]{2,1,0:T(4,128)S(1)}, f32[8,3,64]{2,1,0:T(4,128)S(1)}, u32[]{:S(2)}, u32[]{:S(2)}) collective-permute-start(f32[8,3,64]{2,1,0:T(4,128)S(1)} %get-tuple-element.609), channel_id=1, source_target_pairs={{0,1},{1,2},{2,3},{3,4},{4,5},{5,6},{6,7},{7,0},{8,9},{9,10},{10,1... | collective-permute-start | bytes 18440 | tf_op jit(solution)/shard_map/ppermute | solution.py:40
  47.4 7.9 %collective-permute-start.3 = (f32[8,3,64]{2,1,0:T(4,128)S(1)}, f32[8,3,64]{2,1,0:T(4,128)S(1)}, u32[]{:S(2)}, u32[]{:S(2)}) collective-permute-start(f32[8,3,64]{2,1,0:T(4,128)S(1)} %get-tuple-element.608), channel_id=1, source_target_pairs={{1,0},{2,1},{3,2},{4,3},{5,4},{6,5},{7,6},{0,7},{9,8},{10,9},{11,1... | collective-permute-start | bytes 18440 | tf_op jit(solution)/shard_map/ppermute | solution.py:43
  54.5 1.9 copy-start.2
  56.4 90.5 %copy-start.3 = (f32[2,1,4096]{2,1,0:T(1,128)S(1)}, f32[2,1,4096]{2,1,0:T(1,128)}, u32[]{:S(2)}) copy-start(f32[2,1,4096]{2,1,0:T(1,128)} %param.14) | copy-start | bytes 98308
  167.3 11.2 %collective-permute-start.4 = (f32[2,8,1,4096]{3,2,1,0:T(1,128)S(1)}, f32[2,8,1,4096]{3,2,1,0:T(1,128)S(1)}, u32[]{:S(2)}, u32[]{:S(2)}) collective-permute-start(f32[2,8,1,4096]{3,2,1,0:T(1,128)S(1)} %pad_maximum_fusion.9), channel_id=1, source_target_pairs={{0,8},{8,16},{16,24},{24,32},{32,40},{40,48},{48,56},{56,64},{64,7... | collective-permute-start | bytes 786440 | tf_op jit(solution)/shard_map/ppermute | solution.py:40
  169.3 11.0 %collective-permute-start.5 = (f32[2,8,1,4096]{3,2,1,0:T(1,128)S(1)}, f32[2,8,1,4096]{3,2,1,0:T(1,128)S(1)}, u32[]{:S(2)}, u32[]{:S(2)}) collective-permute-start(f32[2,8,1,4096]{3,2,1,0:T(1,128)S(1)} %pad_maximum_fusion.9), channel_id=1, source_target_pairs={{8,0},{16,8},{24,16},{32,24},{40,32},{48,40},{56,48},{64,56},{72,6... | collective-permute-start | bytes 786440 | tf_op jit(solution)/shard_map/ppermute | solution.py:43
  180.9 10.3 %collective-permute-start.6 = (f32[8,3,64]{2,1,0:T(4,128)S(1)}, f32[8,3,64]{2,1,0:T(4,128)S(1)}, u32[]{:S(2)}, u32[]{:S(2)}) collective-permute-start(f32[8,3,64]{2,1,0:T(4,128)S(1)} %get-tuple-element.607), channel_id=1, source_target_pairs={{0,1},{1,2},{2,3},{3,4},{4,5},{5,6},{6,7},{7,0},{8,9},{9,10},{10,1... | collective-permute-start | bytes 18440 | tf_op jit(solution)/shard_map/ppermute | solution.py:40
  184.1 7.7 %collective-permute-start.7 = (f32[8,3,64]{2,1,0:T(4,128)S(1)}, f32[8,3,64]{2,1,0:T(4,128)S(1)}, u32[]{:S(2)}, u32[]{:S(2)}) collective-permute-start(f32[8,3,64]{2,1,0:T(4,128)S(1)} %get-tuple-element.606), channel_id=1, source_target_pairs={{1,0},{2,1},{3,2},{4,3},{5,4},{6,5},{7,6},{0,7},{9,8},{10,9},{11,1... | collective-permute-start | bytes 18440 | tf_op jit(solution)/shard_map/ppermute | solution.py:43
  192.9 88.7 %copy-start.4 = (s32[1,64]{1,0:T(1,128)S(1)}, s32[1,64]{1,0:T(1,128)}, u32[]{:S(2)}) copy-start(s32[1,64]{1,0:T(1,128)} %param.15) | copy-start | bytes 772
  277.5 23.0 %collective-permute-start.8 = (f32[6,1,2048]{2,1,0:T(1,128)S(1)}, f32[6,1,2048]{2,1,0:T(1,128)S(1)}, u32[]{:S(2)}, u32[]{:S(2)}) collective-permute-start(f32[6,1,2048]{2,1,0:T(1,128)S(1)} %slice.1218), channel_id=1, source_target_pairs={{0,1},{1,2},{2,3},{3,4},{4,5},{5,6},{6,7},{7,0},{8,9},{9,10},{10,1... | collective-permute-start | bytes 147464 | tf_op jit(solution)/shard_map/ppermute | solution.py:50
where the time goes:
time: 304 us; the launch traced here: 303 us
  other arithmetic  156 us (51%)
  starting transfers between devices  51.5 us (17%)
  blocking collectives  32.6 us (11%)
  waiting for transfers between devices  23.6 us (8%)
  loops' own time  20.4 us (7%)
  local copies, waits for them, and re-layouts  11.7 us (4%)
  between operations  6.88 us (2%)
    reduce_sum x12, other arithmetic, one_block(): virial = virial + 0.5 * jnp.sum(magnitude * phys_x * sep_y)  147 us
    all_to_all x2, blocking collectives, sent_to_all(): return lax.all_to_all(copies, axis, split_axis=0, concat_axis=0, tiled=True)  32.6 us
    ppermute x4, starting transfers between devices, with_halo(): lax.ppermute(lax.slice_in_dim(block, 0, width, axis=dim), axis, backward)  31.1 us
    another operation x2, loops' own time, band_forces(): block_forces, block_virials = lax.map(one_block, starts)  20.4 us
    all_to_all x1, waiting for transfers between devices, sent_to_all(): return lax.all_to_all(copies, axis, split_axis=0, concat_axis=0, tiled=True)  15.1 us
    ppermute x4, starting transfers between devices, with_halo(): lax.ppermute(lax.slice_in_dim(block, block.shape[dim] - width, None, axis...  10 us
    all_to_all x1, starting transfers between devices, sent_to_all(): return lax.all_to_all(copies, axis, split_axis=0, concat_axis=0, tiled=True)  6.16 us
  transfers between devices with their start and end apart: 10, of which 7 were waited for; matrix products, arithmetic and copies ran while one was open for 1% of the time, Pallas kernels for 0%

commit v1 on v0

v1 whole, which is shorter than its diff:
```python
import functools

import jax
import jax.numpy as jnp
from jax import lax
from jax.experimental import pallas as pl
from jax.experimental.pallas import tpu as pltpu
from jax.sharding import PartitionSpec as P

TB = 64
LANES = 128
DEPTH = TB / 6.0
INV = 6.0 / TB
REPULSION = 25.0
FRICTION = 4.5
NOISE = 15.0 * 1.4142135623730951
DT = 0.04
RATE = 0.25
FAR = 1.0e6
VSCALE = FRICTION * DEPTH**3
FSCALE = DEPTH**3
WCUT = INV * INV
MESH = pl.DeviceIdType.MESH
f32 = jnp.float32


def body_of(G, F, LP):
    NT = 2 * LP
    NTT = NT * F
    ROWS = 8 * LP
    HP = LP // 2

    def kernel(
        shift_s, strain_s, pos_r, vel_r, cs_r, live_r,
        outp_r, outv_r, stress_r,
        rb, img0, img1, eblk, ecol, jev, jom, jop, facc, fsum, vacc, spos, svel, comb, part,
        ssem, rsem, isend, irecv, fsem, tsend, trecv,
    ):
        g = lax.axis_index("grad")
        f = lax.axis_index("flow")
        up = lax.rem(g + 1, G)
        dn = lax.rem(g + G - 1, G)
        rt = lax.rem(f + 1, F)
        lf = lax.rem(f + F - 1, F)
        first = g == 0
        last = g == G - 1
        img = (img0, img1)
        lane = lax.broadcasted_iota(jnp.int32, (8, LANES), 1)
        sub = lax.broadcasted_iota(jnp.int32, (8, LANES), 0)
        low = lane < TB

        bar = pltpu.get_barrier_semaphore()

        def hello(dg, df):
            pl.semaphore_signal(bar, inc=1, device_id=(dg, df), device_id_type=MESH)

        for k in range(1, F):
            hello(g, lax.rem(f + k, F))

        @pl.when(first)
        def _():
            for k in range(F):
                hello(dn, lax.rem(f + k, F))

        @pl.when(jnp.logical_not(first))
        def _():
            for df in (lf, f, rt):
                hello(dn, df)

        @pl.when(last)
        def _():
            for k in range(F):
                hello(up, lax.rem(f + k, F))

        @pl.when(jnp.logical_not(last))
        def _():
            for df in (lf, f, rt):
                hello(up, df)

        edge = jnp.logical_or(first, last)
        expected = (F - 1) + 6 + jnp.where(edge, F - 3, 0)

        def rcopy(k, ri, pi):
            dg = (up, g, dn)[ri]
            df = (f, rt, lf)[pi]
            src = ((1, LP), (LP, 1), (1, 1))[pi]
            dst = ((1, LP), (0, 1), (LP + 1, 1))[pi]
            return pltpu.make_async_remote_copy(
                src_ref=rb.at[k, 1, pl.ds(*src)],
                dst_ref=rb.at[k, ri, pl.ds(*dst)],
                send_sem=ssem.at[k, ri, pi],
                recv_sem=rsem.at[k, ri, pi],
                device_id=(dg, df),
                device_id_type=MESH,
            )

        def icopy(k, dg, d):
            df = lax.rem(f + d, F)
            return pltpu.make_async_remote_copy(
                src_ref=rb.at[k, 1, pl.ds(1, LP)],
                dst_ref=img[k].at[pl.ds(f * LP, LP)],
                send_sem=isend.at[k, d],
                recv_sem=irecv.at[k, f],
                device_id=(dg, df),
                device_id_type=MESH,
            )

        def iwait(k, d):
            return pltpu.make_async_remote_copy(
                src_ref=rb.at[k, 1, pl.ds(1, LP)],
                dst_ref=img[k].at[pl.ds(d * LP, LP)],
                send_sem=isend.at[k, d],
                recv_sem=irecv.at[k, d],
                device_id=(g, rt),
                device_id_type=MESH,
            )

        def send_rows(k):
            for pi in (1, 2):
                rcopy(k, 1, pi).start()

            @pl.when(first)
            def _():
                for d in range(F):
                    icopy(k, dn, d).start()

            @pl.when(last)
            def _():
                for d in range(F):
                    icopy(k, up, d).start()

            @pl.when(jnp.logical_not(last))
            def _():
                for pi in range(3):
                    rcopy(k, 0, pi).start()

            @pl.when(jnp.logical_not(first))
            def _():
                for pi in range(3):
                    rcopy(k, 2, pi).start()

        def finish_sends(k):
            for pi in (1, 2):
                rcopy(k, 1, pi).wait_send()

            @pl.when(edge)
            def _():
                for d in range(F):
                    icopy(k, dn, d).wait_send()

            @pl.when(jnp.logical_not(last))
            def _():
                for pi in range(3):
                    rcopy(k, 0, pi).wait_send()

            @pl.when(jnp.logical_not(first))
            def _():
                for pi in range(3):
                    rcopy(k, 2, pi).wait_send()

        def write_blocks(k, strain, pos, vel):
            live = live_r[...] > 0.5
            x = (pos[0] + strain * pos[1]) * INV

            def put(field, value):
                rb[k, 1, pl.ds(1, LP), field, :] = value

            def col(field, value):
                eblk[pl.ds(field, LP, stride=8), :] = value

            y, z = pos[1] * INV, pos[2] * INV
            put(0, jnp.where(live, x, FAR))
            col(0, jnp.where(live, x, -FAR))
            put(1, y)
            col(1, y)
            put(2, z)
            col(2, z)
            for i in range(3):
                scaled = vel[i] * VSCALE
                put(3 + i, scaled)
                col(3 + i, scaled)
            cosine, sine = cs_r[2 * k], cs_r[2 * k + 1]
            put(6, cosine)
            col(6, cosine * NOISE)
            put(7, sine)
            col(7, sine * NOISE)

        lane64 = lax.broadcasted_iota(jnp.int32, (TB, LANES), 1)
        low64 = lane64 < TB

        def spread_centres():
            def one(p, carry):
                tile = eblk[pl.ds(pl.multiple_of(p * 8, 8), 8), :]
                turned = tile.T
                for i in range(8):
                    lo = jnp.broadcast_to(turned[:TB, i : i + 1], (TB, LANES))
                    hi = jnp.broadcast_to(turned[TB:, i : i + 1], (TB, LANES))
                    ecol[p, i] = jnp.where(low64, lo, hi)
                return carry

            lax.fori_loop(0, LP, one, 0)

        def offsets(strain, a, b):
            x = (2.0 * b + strain * a) * INV
            y = a * INV
            return jnp.where(sub == 0, x, jnp.where(sub == 1, y, 0.0))

        def halves(left, right):
            return jnp.where(low, pltpu.roll(left, TB, 1), pltpu.roll(right, TB, 1))

        def ready_row(k, ri, strain):
            a = (ri - 1).astype(f32)
            here = offsets(strain, a, 0.0)
            minus = offsets(strain, a, -1.0)
            plus = offsets(strain, a, 1.0)

            def one(q, carry):
                now = rb[k, ri, q]
                nxt = rb[k, ri, q + 1]
                odd = halves(now, nxt)
                at = pl.ds(pl.multiple_of(q * 8, 8), 8)
                jev[at, :] = now + here
                jom[at, :] = odd + minus
                jop[at, :] = odd + plus
                return carry

            lax.fori_loop(0, LP + 1, one, 0)

        def ready_image(k, ri, strain):
            a = (ri - 1).astype(f32)
            here = offsets(strain, a, 0.0)
            minus = offsets(strain, a, -1.0)
            plus = offsets(strain, a, 1.0)
            signed = shift_s[0] * (1 - 2 * lax.div(g, G - 1))

            def one(q, carry):
                tile = lax.rem(NT * f + 2 * q - 2 + signed + 2 * NTT, NTT)
                u = lax.div(tile, 2)
                v = lax.rem(u + 1, NTT // 2)
                one_t = img[k][u]
                two_t = img[k][v]
                mixed = halves(one_t, two_t)
                is_even = jnp.broadcast_to(lax.rem(tile, 2), (8, LANES)) == 0
                now = jnp.where(is_even, one_t, mixed)
                odd = jnp.where(is_even, mixed, two_t)
                at = pl.ds(pl.multiple_of(q * 8, 8), 8)
                jev[at, :] = now + here
                jom[at, :] = odd + minus
                jop[at, :] = odd + plus
                return carry

            lax.fori_loop(0, LP + 1, one, 0)

        def row_pass(k, fresh):
            def one(p, virial):
                def partner(ref, q):
                    base = q * 8
                    return [
                        jnp.broadcast_to(ref[pl.ds(base + i, 1), :], (8, LANES))
                        for i in range(8)
                    ]

                sides = (partner(jom, p), partner(jev, p + 1), partner(jop, p + 1))
                for grp in range(TB // 8):
                    at = pl.ds(grp * 8, 8)
                    ex, ey, ez, eu, ev, ew, ec, es = [ecol[p, i, at, :] for i in range(8)]
                    if fresh:
                        fx = fy = fz = jnp.zeros((8, LANES), f32)
                    else:
                        fx, fy, fz = [facc[p, i, at, :] for i in range(3)]
                    for jx, jy, jz, ju, jv, jw, jc, js in sides:
                        dx = ex - jx
                        dy = ey - jy
                        dz = ez - jz
                        turn = jnp.round(dz)
                        if k > 0:
                            turn = jnp.clip(turn, -1.0, 1.0)
                        dz = dz - turn
                        w = jnp.maximum(WCUT - dx * dx - dy * dy - dz * dz, 0.0)
                        approach = dx * (eu - ju) + dy * (ev - jv) + dz * (ew - jw)
                        kick = REPULSION + (ec * jc + es * js)
                        m = w * (kick - w * approach)
                        mx = m * dx
                        fx = fx + mx
                        fy = fy + m * dy
                        fz = fz + m * dz
                        virial = virial + mx * dy
                    facc[p, 0, at, :] = fx
                    facc[p, 1, at, :] = fy
                    facc[p, 2, at, :] = fz
                return virial

            vacc[...] = lax.fori_loop(0, LP, one, vacc[...])

        def sum_forces():
            for i in range(3):
                fsum[i] = jnp.zeros((TB, LANES), f32)

            def one(p, carry):
                for i in range(3):
                    acc = facc[p, i]
                    lo = jnp.sum(jnp.where(low64, acc, 0.0), axis=1, keepdims=True)
                    hi = jnp.sum(jnp.where(low64, 0.0, acc), axis=1, keepdims=True)
                    now = fsum[i]
                    now = jnp.where(lane64 == p, lo, now)
                    fsum[i] = jnp.where(lane64 == p + LP, hi, now)
                return carry

            lax.fori_loop(0, LP, one, 0)
            forces = []
            lowrow = lax.broadcasted_iota(jnp.int32, (LP, LANES), 1) < TB
            for i in range(3):
                both = jnp.concatenate([fsum[i], fsum[i]], axis=0).T
                forces.append(jnp.where(lowrow, both[:LP], both[LP : 2 * LP]) * FSCALE)
            return forces

        part[F] = jnp.zeros((8, LANES), f32)
        for k in range(2):
            strain = strain_s[0] + k * RATE * DT
            pos = [(pos_r if k == 0 else spos)[i] for i in range(3)]
            vel = [(vel_r if k == 0 else svel)[i] for i in range(3)]
            write_blocks(k, strain, pos, vel)
            if k == 0:
                pl.semaphore_wait(bar, expected)
            send_rows(k)
            spread_centres()
            vacc[...] = jnp.zeros((8, LANES), f32)
            for pi in (1, 2):
                rcopy(k, 1, pi).wait_recv()
            ready_row(k, jnp.int32(1), strain)
            row_pass(k, True)

            @pl.when(jnp.logical_not(first))
            def _():
                for pi in range(3):
                    rcopy(k, 0, pi).wait_recv()
                ready_row(k, jnp.int32(0), strain)

            @pl.when(first)
            def _():
                for pi in range(3):
                    rcopy(k, 2, pi).wait_recv()
                ready_row(k, jnp.int32(2), strain)

            row_pass(k, False)

            @pl.when(jnp.logical_not(edge))
            def _():
                for pi in range(3):
                    rcopy(k, 2, pi).wait_recv()
                ready_row(k, jnp.int32(2), strain)

            @pl.when(edge)
            def _():
                for d in range(F):
                    iwait(k, d).wait_recv()
                ready_image(k, jnp.where(first, 0, 2), strain)

            row_pass(k, False)
            force = sum_forces()
            kinetic = live_r[...] * vel[0] * vel[1]
            folded = kinetic[0:8]
            for q in range(1, LP // 8):
                folded = folded + kinetic[8 * q : 8 * q + 8]
            part[F] = part[F] + folded + vacc[...] * (0.5 * DEPTH**4)
            nvx = vel[0] + DT * (force[0] - RATE * vel[1])
            nvy = vel[1] + DT * force[1]
            nvz = vel[2] + DT * force[2]
            npx = pos[0] + DT * (nvx - strain * nvy)
            npy = pos[1] + DT * nvy
            npz = pos[2] + DT * nvz
            if k == 0:
                for i, value in enumerate((npx, npy, npz)):
                    spos[i] = value
                for i, value in enumerate((nvx, nvy, nvz)):
                    svel[i] = value
            else:
                npx = npx + lax.rem(g, 2).astype(f32) + npy
                for i, value in enumerate((npx, npy, npz, nvx, nvy, nvz)):
                    comb[i, pl.ds(HP, LP), :] = value

        tail = pltpu.make_async_remote_copy(
            src_ref=comb.at[:, pl.ds(LP, HP)],
            dst_ref=comb.at[:, pl.ds(0, HP)],
            send_sem=fsem.at[0],
            recv_sem=fsem.at[1],
            device_id=(g, rt),
            device_id_type=MESH,
        )
        tail.start()

        def share(d):
            return pltpu.make_async_remote_copy(
                src_ref=part.at[F],
                dst_ref=part.at[f],
                send_sem=tsend.at[d],
                recv_sem=trecv.at[f],
                device_id=(g, lax.rem(f + d, F)),
                device_id_type=MESH,
            )

        def shared(d):
            peer = lax.rem(f + d, F)
            return pltpu.make_async_remote_copy(
                src_ref=part.at[F],
                dst_ref=part.at[peer],
                send_sem=tsend.at[d],
                recv_sem=trecv.at[peer],
                device_id=(g, peer),
                device_id_type=MESH,
            )

        for d in range(1, F):
            share(d).start()
        for k in range(2):
            finish_sends(k)
        tail.wait()
        hop = g // 2
        even = lax.rem(hop, 2) == 0
        start = HP - (hop + 1) // 2
        lowrow = lax.broadcasted_iota(jnp.int32, (LP, LANES), 1) < TB

        @pl.when(even)
        def _():
            for i in range(6):
                out = outp_r if i < 3 else outv_r
                out[i % 3] = comb[i, pl.ds(start, LP), :]

        @pl.when(jnp.logical_not(even))
        def _():
            for i in range(6):
                out = outp_r if i < 3 else outv_r
                one = pltpu.roll(comb[i, pl.ds(start, LP), :], TB, 1)
                two = pltpu.roll(comb[i, pl.ds(start + 1, LP), :], TB, 1)
                out[i % 3] = jnp.where(lowrow, one, two)

        total = part[F]
        for d in range(1, F):
            shared(d).wait_recv()
            total = total + part[lax.rem(f + d, F)]
        for d in range(1, F):
            share(d).wait_send()
        whole = jnp.sum(jnp.sum(total, axis=1, keepdims=True), axis=0, keepdims=True)
        stress_r[...] = jnp.broadcast_to(whole * (-1.0 / (2.0 * NTT * 2.0 * DEPTH)), (8, LANES))

    return kernel


def per_device(G, F, bead_pos, bead_vel, noise_angle, occupancy, image_shift, strain):
    width = bead_pos.shape[2]
    LP = width // LANES
    slot = lax.broadcasted_iota(jnp.int32, (1, width), 1) % TB
    live = (slot < jnp.repeat(occupancy, TB, axis=1)).astype(f32).reshape(LP, LANES)
    angle = noise_angle.reshape(2, LP, LANES)
    cs = jnp.stack([jnp.cos(angle), jnp.sin(angle)], 1).reshape(4, LP, LANES)
    vm = pl.BlockSpec(memory_space=pltpu.VMEM)
    sm = pl.BlockSpec(memory_space=pltpu.SMEM)
    rows = 8 * LP
    block = jax.ShapeDtypeStruct((3, LP, LANES), f32)
    dma = pltpu.SemaphoreType.DMA
    newp, newv, stress = pl.pallas_call(
        body_of(G, F, LP),
        out_shape=(block, block, jax.ShapeDtypeStruct((8, LANES), f32)),
        in_specs=[sm, sm, vm, vm, vm, vm],
        out_specs=(vm, vm, vm),
        scratch_shapes=[
            pltpu.VMEM((2, 3, LP + 2, 8, LANES), f32),
            pltpu.VMEM((F * LP, 8, LANES), f32),
            pltpu.VMEM((F * LP, 8, LANES), f32),
            pltpu.VMEM((rows, LANES), f32),
            pltpu.VMEM((LP, 8, TB, LANES), f32),
            pltpu.VMEM((rows + 8, LANES), f32),
            pltpu.VMEM((rows + 8, LANES), f32),
            pltpu.VMEM((rows + 8, LANES), f32),
            pltpu.VMEM((LP, 3, TB, LANES), f32),
            pltpu.VMEM((3, TB, LANES), f32),
            pltpu.VMEM((8, LANES), f32),
            pltpu.VMEM((3, LP, LANES), f32),
            pltpu.VMEM((3, LP, LANES), f32),
            pltpu.VMEM((6, LP + LP // 2, LANES), f32),
            pltpu.VMEM((F + 1, 8, LANES), f32),
            dma((2, 3, 3)),
            dma((2, 3, 3)),
            dma((2, F)),
            dma((2, F)),
            dma((2,)),
            dma((F,)),
            dma((F,)),
        ],
        compiler_params=pltpu.CompilerParams(
            collective_id=0, has_side_effects=True, vmem_limit_bytes=48 * 1024 * 1024
        ),
    )(
        image_shift,
        strain,
        bead_pos.reshape(3, LP, LANES),
        bead_vel.reshape(3, LP, LANES),
        cs,
        live,
    )
    shape = bead_pos.shape
    return newp.reshape(shape), newv.reshape(shape), stress[0, :1]


def solution(mesh):
    G, F = mesh.shape["grad"], mesh.shape["flow"]
    in_specs = (
        P(None, "grad", "flow"),
        P(None, "grad", "flow"),
        P(None, "grad", "flow"),
        P("grad", "flow"),
        P(),
        P(),
    )
    out_specs = (P(None, "grad", "flow"), P(None, "grad", "flow"), P("grad"))
    return jax.shard_map(
        functools.partial(per_device, G, F),
        mesh=mesh,
        in_specs=in_specs,
        out_specs=out_specs,
        check_vma=False,
    )
```

time: 304 us -> 94.4 us (0.31)
  the two profiles are of different devices: /device:TPU:8 before, /device:TPU:4 now
where the time goes in v1:
time: 94.4 us; the launch traced here: 94.1 us
  Pallas kernels  86.3 us (91%)
  local copies, waits for them, and re-layouts  5.07 us (5%)
  between operations  2 us (2%)
    pallas_call x1, Pallas kernels, per_device(): pl.pallas_call(body_of(G, F, LP), out_shape=(block, block, jax.ShapeDtype...  86.3 us
    unnamed x11, local copies, waits for them, and re-layouts  3.33 us

profile of v1, /device:TPU:4, one launch (start us, length us, event | category | flops | bytes accessed | tf_op | source)
XLA Modules:
  0.0 94.1 jit_solution(16413312014214582601)
XLA Ops:
  1.9 0.0 copy-start.3
  1.9 0.5 broadcast.28
  2.4 0.1 copy-done.3
  2.6 0.7 reduce.3
  3.2 0.1 broadcast_in_dim.7
  3.3 0.1 broadcast_in_dim.8
  3.5 0.0 copy-start.2
  3.5 0.1 broadcast_in_dim.9
  3.6 0.6 copy-done.2
  4.2 0.9 %fusion.3 = (f32[2,1,4096]{2,1,0:T(1,128)S(1)}, f32[2,1,4096]{2,1,0:T(1,128)S(1)}) fusion(f32[2,1,4096]{2,1,0:T(1,128)S(1)} %copy-done.2), kind=kLoop, calls=%fused_computation.7 | loop fusion | bytes 98304 | tf_op jit(solution)/shard_map/cos | solution.py:455
  5.2 0.0 copy-start
  5.2 0.0 copy-start.1
  5.2 0.8 copy-done
  6.0 0.0 copy-done.1
  6.0 86.3 %shard_map.85 = (f32[3,32,128]{2,1,0:T(8,128)S(1)}, f32[3,32,128]{2,1,0:T(8,128)S(1)}, f32[8,128]{1,0:T(8,128)S(1)}) custom-call(s32[1]{0:T(128)S(6)} %copy.19.shift_s, f32[1]{0:T(128)S(6)} %copy.20.strain_s, f32[3,32,128]{2,1,0:T(8,128)S(1)} %bitcast.15, f32[3,32,128]{2,1,0:T(8,128)S(1)} %bitcast.16, f32[4,32,128]{2,1,0:T(8,128)S(1)} %bitcast.12, ...), custom_call_target="tpu_custom_call" | custom-call | tf_op jit(solution)/shard_map/pallas_call | solution.py:461
  92.4 0.5 slice.3
  92.9 0.6 copy.21
  93.5 0.6 copy.22
  (2 shorter events, 0.0 us)
Async XLA Ops:
  1.9 0.7 copy-start.3
  3.5 0.8 copy-start.2
  5.2 0.8 copy-start
  5.2 0.8 copy-start.1

commit v2 on v1

--- a/solution.py
+++ b/solution.py
@@ -17,6 +17,7 @@
 DT = 0.04
 RATE = 0.25
 FAR = 1.0e6
+TERMS = 48
 VSCALE = FRICTION * DEPTH**3
 FSCALE = DEPTH**3
 WCUT = INV * INV
@@ -31,9 +32,9 @@
     HP = LP // 2
 
     def kernel(
-        shift_s, strain_s, pos_r, vel_r, cs_r, live_r,
+        shift_s, strain_s, pos_r, vel_r, angle_r, occ_r,
         outp_r, outv_r, stress_r,
-        rb, img0, img1, eblk, ecol, jev, jom, jop, facc, fsum, vacc, spos, svel, comb, part,
+        rb, img0, img1, eblk, weights, live_v, cs_v, ecol, jev, jom, jop, facc, picks, vacc, spos, svel, comb, part,
         ssem, rsem, isend, irecv, fsem, tsend, trecv,
     ):
         g = lax.axis_index("grad")
@@ -159,46 +160,55 @@
                     rcopy(k, 2, pi).wait_send()
 
         def write_blocks(k, strain, pos, vel):
-            live = live_r[...] > 0.5
+            live = live_v[...] > 0.5
             x = (pos[0] + strain * pos[1]) * INV
 
             def put(field, value):
                 rb[k, 1, pl.ds(1, LP), field, :] = value
 
             def col(field, value):
-                eblk[pl.ds(field, LP, stride=8), :] = value
+                rest = value
+                for term in range(3):
+                    piece = rest.astype(jnp.bfloat16).astype(f32)
+                    rest = rest - piece
+                    for half in range(2):
+                        turned = pltpu.roll(piece, TB, 1) if half else piece
+                        eblk[pl.ds(term * 16 + half * 8 + field, LP, stride=TERMS), :] = turned
 
             y, z = pos[1] * INV, pos[2] * INV
-            put(0, jnp.where(live, x, FAR))
-            col(0, jnp.where(live, x, -FAR))
-            put(1, y)
-            col(1, y)
-            put(2, z)
-            col(2, z)
-            for i in range(3):
-                scaled = vel[i] * VSCALE
-                put(3 + i, scaled)
-                col(3 + i, scaled)
-            cosine, sine = cs_r[2 * k], cs_r[2 * k + 1]
-            put(6, cosine)
-            col(6, cosine * NOISE)
-            put(7, sine)
-            col(7, sine * NOISE)
-
-        lane64 = lax.broadcasted_iota(jnp.int32, (TB, LANES), 1)
-        low64 = lane64 < TB
+            cosine, sine = cs_v[2 * k], cs_v[2 * k + 1]
+            scaled = [vel[i] * VSCALE for i in range(3)]
+            for field, value in enumerate((jnp.where(live, x, FAR), y, z, *scaled, cosine, sine)):
+                put(field, value)
+
+            def columns():
+                left = (jnp.where(live, x, -FAR), y, z, *scaled, cosine * NOISE, sine * NOISE)
+                for field, value in enumerate(left):
+                    col(field, value)
+
+            return columns
+
+        def fill_weights():
+            row = lax.broadcasted_iota(jnp.int32, (TERMS, 8 * LANES), 0)
+            column = lax.broadcasted_iota(jnp.int32, (TERMS, 8 * LANES), 1)
+            same = lax.rem(row, 16) == lax.rem(column // TB, 2) * 8 + column // LANES
+            weights[...] = same.astype(f32).astype(jnp.bfloat16)
 
         def spread_centres():
-            def one(p, carry):
-                tile = eblk[pl.ds(pl.multiple_of(p * 8, 8), 8), :]
-                turned = tile.T
-                for i in range(8):
-                    lo = jnp.broadcast_to(turned[:TB, i : i + 1], (TB, LANES))
-                    hi = jnp.broadcast_to(turned[TB:, i : i + 1], (TB, LANES))
-                    ecol[p, i] = jnp.where(low64, lo, hi)
+            step = 4 if LP % 4 == 0 else 1
+
+            def some(c, carry):
+                turned = []
+                for j in range(step):
+                    at = pl.ds(pl.multiple_of((c * step + j) * TERMS, TERMS), TERMS)
+                    turned.append(eblk[at, :].T[:TB].astype(jnp.bfloat16))
+                for j in range(step):
+                    ecol[c * step + j] = jnp.dot(
+                        turned[j], weights[...], preferred_element_type=f32
+                    )
                 return carry
 
-            lax.fori_loop(0, LP, one, 0)
+            lax.fori_loop(0, LP // step, some, 0)
 
         def offsets(strain, a, b):
             x = (2.0 * b + strain * a) * INV
@@ -207,6 +217,16 @@
 
         def halves(left, right):
             return jnp.where(low, pltpu.roll(left, TB, 1), pltpu.roll(right, TB, 1))
+
+        def several(one):
+            step = 11 if (LP + 1) % 11 == 0 else 1
+
+            def some(c, carry):
+                for j in range(step):
+                    one(c * step + j)
+                return carry
+
+            lax.fori_loop(0, (LP + 1) // step, some, 0)
 
         def ready_row(k, ri, strain):
             a = (ri - 1).astype(f32)
@@ -214,7 +234,7 @@
             minus = offsets(strain, a, -1.0)
             plus = offsets(strain, a, 1.0)
 
-            def one(q, carry):
+            def one(q):
                 now = rb[k, ri, q]
                 nxt = rb[k, ri, q + 1]
                 odd = halves(now, nxt)
@@ -222,9 +242,8 @@
                 jev[at, :] = now + here
                 jom[at, :] = odd + minus
                 jop[at, :] = odd + plus
-                return carry
-
-            lax.fori_loop(0, LP + 1, one, 0)
+
+            several(one)
 
         def ready_image(k, ri, strain):
             a = (ri - 1).astype(f32)
@@ -233,7 +252,7 @@
             plus = offsets(strain, a, 1.0)
             signed = shift_s[0] * (1 - 2 * lax.div(g, G - 1))
 
-            def one(q, carry):
+            def one(q):
                 tile = lax.rem(NT * f + 2 * q - 2 + signed + 2 * NTT, NTT)
                 u = lax.div(tile, 2)
                 v = lax.rem(u + 1, NTT // 2)
@@ -247,9 +266,8 @@
                 jev[at, :] = now + here
                 jom[at, :] = odd + minus
                 jop[at, :] = odd + plus
-                return carry
-
-            lax.fori_loop(0, LP + 1, one, 0)
+
+            several(one)
 
         def row_pass(k, fresh):
             def one(p, virial):
@@ -260,14 +278,15 @@
                         for i in range(8)
                     ]
 
+                wide = pl.ds(pl.multiple_of(p * LANES, LANES), LANES)
                 sides = (partner(jom, p), partner(jev, p + 1), partner(jop, p + 1))
                 for grp in range(TB // 8):
                     at = pl.ds(grp * 8, 8)
-                    ex, ey, ez, eu, ev, ew, ec, es = [ecol[p, i, at, :] for i in range(8)]
+                    ex, ey, ez, eu, ev, ew, ec, es = [ecol[p, at, pl.ds(i * LANES, LANES)] for i in range(8)]
                     if fresh:
                         fx = fy = fz = jnp.zeros((8, LANES), f32)
                     else:
-                        fx, fy, fz = [facc[p, i, at, :] for i in range(3)]
+                        fx, fy, fz = [facc[pl.ds(i * TB + grp * 8, 8), wide] for i in range(3)]
                     for jx, jy, jz, ju, jv, jw, jc, js in sides:
                         dx = ex - jx
                         dy = ey - jy
@@ -285,44 +304,68 @@
                         fy = fy + m * dy
                         fz = fz + m * dz
                         virial = virial + mx * dy
-                    facc[p, 0, at, :] = fx
-                    facc[p, 1, at, :] = fy
-                    facc[p, 2, at, :] = fz
+                    facc[pl.ds(0 * TB + grp * 8, 8), wide] = fx
+                    facc[pl.ds(1 * TB + grp * 8, 8), wide] = fy
+                    facc[pl.ds(2 * TB + grp * 8, 8), wide] = fz
                 return virial
 
             vacc[...] = lax.fori_loop(0, LP, one, vacc[...])
 
+        lowrow = lax.broadcasted_iota(jnp.int32, (LP, LANES), 1) < TB
+
+        def fill_picks():
+            tile = lax.broadcasted_iota(jnp.int32, (LANES, LANES), 0) // TB * LP
+            column = lax.broadcasted_iota(jnp.int32, (LANES, LANES), 1) - tile
+
+            def one(p, carry):
+                at = pl.ds(pl.multiple_of(p * LANES, LANES), LANES)
+                picks[at, :] = (column == p).astype(f32).astype(jnp.bfloat16)
+                return carry
+
+            lax.fori_loop(0, LP, one, 0)
+
         def sum_forces():
+            acc = facc[...]
+            big = acc.astype(jnp.bfloat16)
+            small = (acc - big.astype(f32)).astype(jnp.bfloat16)
+            pick = picks[...]
+            summed = jnp.dot(big, pick, preferred_element_type=f32)
+            summed = summed + jnp.dot(small, pick, preferred_element_type=f32)
+            forces = []
             for i in range(3):
-                fsum[i] = jnp.zeros((TB, LANES), f32)
-
-            def one(p, carry):
-                for i in range(3):
-                    acc = facc[p, i]
-                    lo = jnp.sum(jnp.where(low64, acc, 0.0), axis=1, keepdims=True)
-                    hi = jnp.sum(jnp.where(low64, 0.0, acc), axis=1, keepdims=True)
-                    now = fsum[i]
-                    now = jnp.where(lane64 == p, lo, now)
-                    fsum[i] = jnp.where(lane64 == p + LP, hi, now)
-                return carry
-
-            lax.fori_loop(0, LP, one, 0)
-            forces = []
-            lowrow = lax.broadcasted_iota(jnp.int32, (LP, LANES), 1) < TB
-            for i in range(3):
-                both = jnp.concatenate([fsum[i], fsum[i]], axis=0).T
+                part_i = summed[i * TB : (i + 1) * TB]
+                both = jnp.concatenate([part_i, part_i], axis=0).T
                 forces.append(jnp.where(lowrow, both[:LP], both[LP : 2 * LP]) * FSCALE)
             return forces
 
         part[F] = jnp.zeros((8, LANES), f32)
+        tile_of = lax.broadcasted_iota(jnp.int32, (LP, NT), 1)
+        row_of = lax.broadcasted_iota(jnp.int32, (LP, NT), 0)
+        counts = jnp.broadcast_to(occ_r[...].astype(f32), (LP, NT))
+        counts = jnp.where(tile_of // 2 == row_of, counts, 0.0).astype(jnp.bfloat16)
+        side = lax.rem(lax.broadcasted_iota(jnp.int32, (NT, LANES), 0), 2)
+        half = lax.broadcasted_iota(jnp.int32, (NT, LANES), 1) // TB
+        limit = jnp.dot(
+            counts, (side == half).astype(f32).astype(jnp.bfloat16), preferred_element_type=f32
+        )
+        slot = lax.rem(lax.broadcasted_iota(jnp.int32, (LP, LANES), 1), TB).astype(f32)
+        live_v[...] = (slot < limit).astype(f32)
+        cs_v[0] = jnp.cos(angle_r[0])
+        cs_v[1] = jnp.sin(angle_r[0])
         for k in range(2):
             strain = strain_s[0] + k * RATE * DT
             pos = [(pos_r if k == 0 else spos)[i] for i in range(3)]
             vel = [(vel_r if k == 0 else svel)[i] for i in range(3)]
-            write_blocks(k, strain, pos, vel)
+            columns = write_blocks(k, strain, pos, vel)
             if k == 0:
                 pl.semaphore_wait(bar, expected)
             send_rows(k)
+            if k == 0:
+                cs_v[2] = jnp.cos(angle_r[1])
+                cs_v[3] = jnp.sin(angle_r[1])
+                fill_picks()
+                fill_weights()
+            columns()
             spread_centres()
             vacc[...] = jnp.zeros((8, LANES), f32)
             for pi in (1, 2):
@@ -334,14 +377,13 @@
             def _():
                 for pi in range(3):
                     rcopy(k, 0, pi).wait_recv()
-                ready_row(k, jnp.int32(0), strain)
 
             @pl.when(first)
             def _():
                 for pi in range(3):
                     rcopy(k, 2, pi).wait_recv()
-                ready_row(k, jnp.int32(2), strain)
-
+
+            ready_row(k, jnp.where(first, 2, 0), strain)
             row_pass(k, False)
 
             @pl.when(jnp.logical_not(edge))
@@ -358,7 +400,7 @@
 
             row_pass(k, False)
             force = sum_forces()
-            kinetic = live_r[...] * vel[0] * vel[1]
+            kinetic = live_v[...] * vel[0] * vel[1]
             folded = kinetic[0:8]
             for q in range(1, LP // 8):
                 folded = folded + kinetic[8 * q : 8 * q + 8]
@@ -418,7 +460,6 @@
         hop = g // 2
         even = lax.rem(hop, 2) == 0
         start = HP - (hop + 1) // 2
-        lowrow = lax.broadcasted_iota(jnp.int32, (LP, LANES), 1) < TB
 
         @pl.when(even)
         def _():
@@ -449,10 +490,6 @@
 def per_device(G, F, bead_pos, bead_vel, noise_angle, occupancy, image_shift, strain):
     width = bead_pos.shape[2]
     LP = width // LANES
-    slot = lax.broadcasted_iota(jnp.int32, (1, width), 1) % TB
-    live = (slot < jnp.repeat(occupancy, TB, axis=1)).astype(f32).reshape(LP, LANES)
-    angle = noise_angle.reshape(2, LP, LANES)
-    cs = jnp.stack([jnp.cos(angle), jnp.sin(angle)], 1).reshape(4, LP, LANES)
     vm = pl.BlockSpec(memory_space=pltpu.VMEM)
     sm = pl.BlockSpec(memory_space=pltpu.SMEM)
     rows = 8 * LP
@@ -467,13 +504,16 @@
             pltpu.VMEM((2, 3, LP + 2, 8, LANES), f32),
             pltpu.VMEM((F * LP, 8, LANES), f32),
             pltpu.VMEM((F * LP, 8, LANES), f32),
-            pltpu.VMEM((rows, LANES), f32),
-            pltpu.VMEM((LP, 8, TB, LANES), f32),
+            pltpu.VMEM((LP * TERMS, LANES), f32),
+            pltpu.VMEM((TERMS, 8 * LANES), jnp.bfloat16),
+            pltpu.VMEM((LP, LANES), f32),
+            pltpu.VMEM((4, LP, LANES), f32),
+            pltpu.VMEM((LP, TB, 8 * LANES), f32),
             pltpu.VMEM((rows + 8, LANES), f32),
             pltpu.VMEM((rows + 8, LANES), f32),
             pltpu.VMEM((rows + 8, LANES), f32),
-            pltpu.VMEM((LP, 3, TB, LANES), f32),
-            pltpu.VMEM((3, TB, LANES), f32),
+            pltpu.VMEM((3 * TB, LP * LANES), f32),
+            pltpu.VMEM((LP * LANES, LANES), jnp.bfloat16),
             pltpu.VMEM((8, LANES), f32),
             pltpu.VMEM((3, LP, LANES), f32),
             pltpu.VMEM((3, LP, LANES), f32),
@@ -495,8 +535,8 @@
         strain,
         bead_pos.reshape(3, LP, LANES),
         bead_vel.reshape(3, LP, LANES),
-        cs,
-        live,
+        noise_angle.reshape(2, LP, LANES),
+        occupancy,
     )
     shape = bead_pos.shape
     return newp.reshape(shape), newv.reshape(shape), stress[0, :1]

time: 94.4 us -> 68.7 us (0.73)
  the two profiles are of different devices: /device:TPU:4 before, /device:TPU:16 now
where the time goes in v2:
time: 68.7 us; the launch traced here: 68.4 us
  Pallas kernels  61.7 us (90%)
  local copies, waits for them, and re-layouts  4.75 us (7%)
  between operations  1.94 us (3%)
    pallas_call x1, Pallas kernels, per_device(): pl.pallas_call(body_of(G, F, LP), out_shape=(block, block, jax.ShapeDtype...  61.7 us
    unnamed x10, local copies, waits for them, and re-layouts  4.24 us

profile of v2, /device:TPU:16, one launch (start us, length us, event | category | flops | bytes accessed | tf_op | source)
XLA Modules:
  0.0 68.4 jit_solution(1286693697653838442)
XLA Ops:
  1.9 0.0 copy-start.3
  1.9 0.6 copy-done.3
  2.6 0.0 copy-start
  2.6 0.8 %copy-done = f32[3,1,4096]{2,1,0:T(1,128)S(1)} copy-done((f32[3,1,4096]{2,1,0:T(1,128)S(1)}, f32[3,1,4096]{2,1,0:T(1,128)}, u32[]{:S(2)}) %copy-start) | copy-done | bytes 49176
  3.4 0.0 copy-start.1
  3.4 0.8 %copy-done.1 = f32[3,1,4096]{2,1,0:T(1,128)S(1)} copy-done((f32[3,1,4096]{2,1,0:T(1,128)S(1)}, f32[3,1,4096]{2,1,0:T(1,128)}, u32[]{:S(2)}) %copy-start.1) | copy-done | bytes 49176
  4.2 0.0 copy-start.2
  4.2 0.8 %copy-done.2 = f32[2,1,4096]{2,1,0:T(1,128)S(1)} copy-done((f32[2,1,4096]{2,1,0:T(1,128)S(1)}, f32[2,1,4096]{2,1,0:T(1,128)}, u32[]{:S(2)}) %copy-start.2) | copy-done | bytes 32792
  4.9 61.7 %shard_map.85 = (f32[3,32,128]{2,1,0:T(8,128)S(1)}, f32[3,32,128]{2,1,0:T(8,128)S(1)}, f32[8,128]{1,0:T(8,128)S(1)}) custom-call(s32[1]{0:T(128)S(6)} %copy.15.shift_s, f32[1]{0:T(128)S(6)} %copy.16.strain_s, f32[3,32,128]{2,1,0:T(8,128)S(1)} %bitcast.6, f32[3,32,128]{2,1,0:T(8,128)S(1)} %bitcast.7, f32[2,32,128]{2,1,0:T(8,128)S(1)} %bitcast.10, ...), custom_call_target="tpu_custom_call" | custom-call | tf_op jit(solution)/shard_map/pallas_call | solution.py:498
  66.7 0.5 slice.3
  67.2 0.6 copy.17
  67.8 0.6 copy.18
Async XLA Ops:
  1.9 0.7 copy-start.3
  2.6 0.8 %copy-start = (f32[3,1,4096]{2,1,0:T(1,128)S(1)}, f32[3,1,4096]{2,1,0:T(1,128)}, u32[]{:S(2)}) copy-start(f32[3,1,4096]{2,1,0:T(1,128)} %param.6) | copy-start | bytes 147460
  3.4 0.8 %copy-start.1 = (f32[3,1,4096]{2,1,0:T(1,128)S(1)}, f32[3,1,4096]{2,1,0:T(1,128)}, u32[]{:S(2)}) copy-start(f32[3,1,4096]{2,1,0:T(1,128)} %param.7) | copy-start | bytes 147460
  4.2 0.8 %copy-start.2 = (f32[2,1,4096]{2,1,0:T(1,128)S(1)}, f32[2,1,4096]{2,1,0:T(1,128)}, u32[]{:S(2)}) copy-start(f32[2,1,4096]{2,1,0:T(1,128)} %param.8) | copy-start | bytes 98308

commit v3 on v2

--- a/solution.py
+++ b/solution.py
@@ -18,6 +18,7 @@
 RATE = 0.25
 FAR = 1.0e6
 TERMS = 48
+SPAN = 4
 VSCALE = FRICTION * DEPTH**3
 FSCALE = DEPTH**3
 WCUT = INV * INV
@@ -25,7 +26,7 @@
 f32 = jnp.float32
 
 
-def body_of(G, F, LP):
+def body_of(G, F, LP, QLO, NQ):
     NT = 2 * LP
     NTT = NT * F
     ROWS = 8 * LP
@@ -95,24 +96,41 @@
                 device_id_type=MESH,
             )
 
-        def icopy(k, dg, d):
-            df = lax.rem(f + d, F)
+        offs = [(d, d < 0) for d in range(-1, NQ + 1)]
+
+        def icopy(k, d):
+            hop = QLO + offs[d][0]
+            df = lax.rem(f + jnp.where(first, hop, -hop) + 2 * F, F)
+            dg = jnp.where(first, dn, up)
+            if offs[d][1]:
+                at = jnp.where(first, 0, LP - 1)
+                count = 1
+            else:
+                at, count = 0, LP
             return pltpu.make_async_remote_copy(
-                src_ref=rb.at[k, 1, pl.ds(1, LP)],
-                dst_ref=img[k].at[pl.ds(f * LP, LP)],
+                src_ref=rb.at[k, 1, pl.ds(1 + at, count)],
+                dst_ref=img[k].at[pl.ds(f * LP + at, count)],
                 send_sem=isend.at[k, d],
-                recv_sem=irecv.at[k, f],
+                recv_sem=irecv.at[k, d],
                 device_id=(dg, df),
                 device_id_type=MESH,
             )
 
         def iwait(k, d):
+            hop = QLO + offs[d][0]
+            df = lax.rem(f + jnp.where(first, hop, -hop) + 2 * F, F)
+            dg = jnp.where(first, dn, up)
+            if offs[d][1]:
+                at = jnp.where(first, LP - 1, 0)
+                count = 1
+            else:
+                at, count = 0, LP
             return pltpu.make_async_remote_copy(
-                src_ref=rb.at[k, 1, pl.ds(1, LP)],
-                dst_ref=img[k].at[pl.ds(d * LP, LP)],
+                src_ref=rb.at[k, 1, pl.ds(1 + at, count)],
+                dst_ref=img[k].at[pl.ds(df * LP + at, count)],
                 send_sem=isend.at[k, d],
                 recv_sem=irecv.at[k, d],
-                device_id=(g, rt),
+                device_id=(dg, df),
                 device_id_type=MESH,
             )
 
@@ -120,15 +138,10 @@
             for pi in (1, 2):
                 rcopy(k, 1, pi).start()
 
-            @pl.when(first)
-            def _():
-                for d in range(F):
-                    icopy(k, dn, d).start()
-
-            @pl.when(last)
-            def _():
-                for d in range(F):
-                    icopy(k, up, d).start()
+            @pl.when(edge)
+            def _():
+                for d in range(NQ + 2):
+                    icopy(k, d).start()
 
             @pl.when(jnp.logical_not(last))
             def _():
@@ -146,8 +159,8 @@
 
             @pl.when(edge)
             def _():
-                for d in range(F):
-                    icopy(k, dn, d).wait_send()
+                for d in range(NQ + 2):
+                    icopy(k, d).wait_send()
 
             @pl.when(jnp.logical_not(last))
             def _():
@@ -394,7 +407,7 @@
 
             @pl.when(edge)
             def _():
-                for d in range(F):
+                for d in range(NQ + 2):
                     iwait(k, d).wait_recv()
                 ready_image(k, jnp.where(first, 0, 2), strain)
 
@@ -475,10 +488,12 @@
                 two = pltpu.roll(comb[i, pl.ds(start + 1, LP), :], TB, 1)
                 out[i % 3] = jnp.where(lowrow, one, two)
 
-        total = part[F]
         for d in range(1, F):
             shared(d).wait_recv()
-            total = total + part[lax.rem(f + d, F)]
+        part[f] = part[F]
+        total = part[0]
+        for d in range(1, F):
+            total = total + part[d]
         for d in range(1, F):
             share(d).wait_send()
         whole = jnp.sum(jnp.sum(total, axis=1, keepdims=True), axis=0, keepdims=True)
@@ -495,8 +510,9 @@
     rows = 8 * LP
     block = jax.ShapeDtypeStruct((3, LP, LANES), f32)
     dma = pltpu.SemaphoreType.DMA
-    newp, newv, stress = pl.pallas_call(
-        body_of(G, F, LP),
+    NQ = SPAN
+    call = lambda branch: pl.pallas_call(
+        body_of(G, F, LP, branch * NQ, NQ),
         out_shape=(block, block, jax.ShapeDtypeStruct((8, LANES), f32)),
         in_specs=[sm, sm, vm, vm, vm, vm],
         out_specs=(vm, vm, vm),
@@ -521,16 +537,17 @@
             pltpu.VMEM((F + 1, 8, LANES), f32),
             dma((2, 3, 3)),
             dma((2, 3, 3)),
-            dma((2, F)),
-            dma((2, F)),
+            dma((2, NQ + 2)),
+            dma((2, NQ + 2)),
             dma((2,)),
             dma((F,)),
             dma((F,)),
         ],
         compiler_params=pltpu.CompilerParams(
-            collective_id=0, has_side_effects=True, vmem_limit_bytes=48 * 1024 * 1024
+            collective_id=branch, has_side_effects=True, vmem_limit_bytes=48 * 1024 * 1024
         ),
-    )(
+    )
+    args = (
         image_shift,
         strain,
         bead_pos.reshape(3, LP, LANES),
@@ -538,6 +555,8 @@
         noise_angle.reshape(2, LP, LANES),
         occupancy,
     )
+    branches = [call(branch) for branch in range(F // NQ)]
+    newp, newv, stress = lax.switch(image_shift[0] // (2 * LP * NQ), branches, *args)
     shape = bead_pos.shape
     return newp.reshape(shape), newv.reshape(shape), stress[0, :1]
 

time: 68.7 us -> 60.9 us (0.89)
  the two profiles are of different devices: /device:TPU:16 before, /device:TPU:2 now
where the time goes in v3:
time: 60.9 us; the launch traced here: 60.6 us
  Pallas kernels  56.9 us (93%)
  local copies, waits for them, and re-layouts  2.41 us (4%)
  between operations  1.34 us (2%)
    pallas_call x1, Pallas kernels, per_device(): lax.switch(image_shift[0] // (2 * LP * NQ), branches, *args)  56.9 us
    unnamed x6, local copies, waits for them, and re-layouts  1.89 us

profile of v3, /device:TPU:2, one launch (start us, length us, event | category | flops | bytes accessed | tf_op | source)
XLA Modules:
  0.0 60.6 jit_solution(18106724382082779658)
XLA Ops:
  0.6 0.0 copy-start
  1.3 0.0 copy-start.1
  1.3 0.1 copy-done
  1.4 0.6 copy-done.1
  2.0 56.9 %conditional.1 = ((f32[3,32,128]{2,1,0:T(8,128)S(1)}, f32[3,32,128]{2,1,0:T(8,128)S(1)}, f32[8,128]{1,0:T(8,128)S(1)})) conditional(s32[]{:T(128)} %clamp.3, (s32[1]{0:T(128)}, f32[1]{0:T(128)}, f32[3,32,128]{2,1,0:T(8,128)}, f32[3,32,128]{2,1,0:T(8,128)}, f32[2,32,128]{2,1,0:T(8,128)S(1)}, /*index=5*/s32[1,64]{1,0:T(1,128)S(1)}) %tuple.37, ...), branch_computations={%region_0.1_spmd, %region_1.2_spmd} | conditional | bytes 8 | solution.py:559
  2.0 56.9 %branch_1_fun.1 = (f32[3,32,128]{2,1,0:T(8,128)S(1)}, f32[3,32,128]{2,1,0:T(8,128)S(1)}, f32[8,128]{1,0:T(8,128)S(1)}) custom-call(s32[1]{0:T(128)} %get-tuple-element.42.shift_s, f32[1]{0:T(128)} %get-tuple-element.43.strain_s, f32[3,32,128]{2,1,0:T(8,128)} %get-tuple-element.44.pos_r, f32[3,32,128]{2,1,0:T(8,128)} %get-tuple-element.45.vel_r, ...), custom_call_target="tpu_custom_call" | custom-call | tf_op jit(solution)/shard_map/cond/branch_1_fun/pallas_call | solution.py:559
  58.9 0.5 slice.7
  59.4 0.6 %copy.18 = f32[3,1,4096]{2,1,0:T(1,128)} copy(f32[3,1,4096]{2,1,0:T(1,128)S(1)} %bitcast.17) | data formatting | bytes 98304
  60.0 0.6 %copy.19 = f32[3,1,4096]{2,1,0:T(1,128)} copy(f32[3,1,4096]{2,1,0:T(1,128)S(1)} %bitcast.18) | data formatting | bytes 98304
Async XLA Ops:
  0.6 0.8 %copy-start = (f32[2,1,4096]{2,1,0:T(1,128)S(1)}, f32[2,1,4096]{2,1,0:T(1,128)}, u32[]{:S(2)}) copy-start(f32[2,1,4096]{2,1,0:T(1,128)} %param.10) | copy-start | bytes 98308
  1.3 0.7 %copy-start.1 = (s32[1,64]{1,0:T(1,128)S(1)}, s32[1,64]{1,0:T(1,128)}, u32[]{:S(2)}) copy-start(s32[1,64]{1,0:T(1,128)} %param.11) | copy-start | bytes 772

commit v4 on v3

--- a/solution.py
+++ b/solution.py
@@ -231,17 +231,17 @@
         def halves(left, right):
             return jnp.where(low, pltpu.roll(left, TB, 1), pltpu.roll(right, TB, 1))
 
-        def several(one):
-            step = 11 if (LP + 1) % 11 == 0 else 1
+        def several(one, low_q=0, count=LP + 1):
+            step = 11 if count % 11 == 0 else count
 
             def some(c, carry):
                 for j in range(step):
-                    one(c * step + j)
+                    one(low_q + c * step + j)
                 return carry
 
-            lax.fori_loop(0, (LP + 1) // step, some, 0)
-
-        def ready_row(k, ri, strain):
+            lax.fori_loop(0, count // step, some, 0)
+
+        def ready_row(k, ri, strain, stage=None):
             a = (ri - 1).astype(f32)
             here = offsets(strain, a, 0.0)
             minus = offsets(strain, a, -1.0)
@@ -251,12 +251,19 @@
                 now = rb[k, ri, q]
                 nxt = rb[k, ri, q + 1]
                 odd = halves(now, nxt)
-                at = pl.ds(pl.multiple_of(q * 8, 8), 8)
+                at = pl.ds(q * 8 if isinstance(q, int) else pl.multiple_of(q * 8, 8), 8)
                 jev[at, :] = now + here
                 jom[at, :] = odd + minus
                 jop[at, :] = odd + plus
 
-            several(one)
+            if stage is None:
+                several(one)
+            elif stage == 0:
+                several(one, 1, LP - 1)
+                jev[pl.ds(8 * LP, 8), :] = rb[k, ri, LP] + here
+            else:
+                one(0)
+                one(LP)
 
         def ready_image(k, ri, strain):
             a = (ri - 1).astype(f32)
@@ -282,8 +289,12 @@
 
             several(one)
 
-        def row_pass(k, fresh):
-            def one(p, virial):
+        def row_pass(k, fresh, pairs=None):
+            count, first_p, stride = pairs or (LP, 0, 1)
+
+            def one(n, virial):
+                p = first_p + n * stride
+
                 def partner(ref, q):
                     base = q * 8
                     return [
@@ -322,7 +333,7 @@
                     facc[pl.ds(2 * TB + grp * 8, 8), wide] = fz
                 return virial
 
-            vacc[...] = lax.fori_loop(0, LP, one, vacc[...])
+            vacc[...] = lax.fori_loop(0, count, one, vacc[...])
 
         lowrow = lax.broadcasted_iota(jnp.int32, (LP, LANES), 1) < TB
 
@@ -381,10 +392,12 @@
             columns()
             spread_centres()
             vacc[...] = jnp.zeros((8, LANES), f32)
+            ready_row(k, jnp.int32(1), strain, 0)
+            row_pass(k, True, (LP - 2, 1, 1))
             for pi in (1, 2):
                 rcopy(k, 1, pi).wait_recv()
-            ready_row(k, jnp.int32(1), strain)
-            row_pass(k, True)
+            ready_row(k, jnp.int32(1), strain, 1)
+            row_pass(k, True, (2, 0, LP - 1))
 
             @pl.when(jnp.logical_not(first))
             def _():

time: 60.9 us -> 59.1 us (0.970)
  the two profiles are of different devices: /device:TPU:2 before, /device:TPU:4 now
where the time goes in v4:
time: 59.1 us; the launch traced here: 58.8 us
  Pallas kernels  55.1 us (93%)
  local copies, waits for them, and re-layouts  2.41 us (4%)
  between operations  1.34 us (2%)
    pallas_call x1, Pallas kernels, per_device(): lax.switch(image_shift[0] // (2 * LP * NQ), branches, *args)  55.1 us
    unnamed x6, local copies, waits for them, and re-layouts  1.89 us

profile of v4, /device:TPU:4, one launch (start us, length us, event | category | flops | bytes accessed | tf_op | source)
XLA Modules:
  0.0 58.8 jit_solution(14734500694929353179)
XLA Ops:
  0.6 0.0 copy-start
  1.3 0.0 copy-start.1
  1.3 0.1 copy-done
  1.4 0.6 %copy-done.1 = s32[1,64]{1,0:T(1,128)S(1)} copy-done((s32[1,64]{1,0:T(1,128)S(1)}, s32[1,64]{1,0:T(1,128)}, u32[]{:S(2)}) %copy-start.1) | copy-done | bytes 280
  2.0 55.1 %conditional.1 = ((f32[3,32,128]{2,1,0:T(8,128)S(1)}, f32[3,32,128]{2,1,0:T(8,128)S(1)}, f32[8,128]{1,0:T(8,128)S(1)})) conditional(s32[]{:T(128)} %clamp.3, (s32[1]{0:T(128)}, f32[1]{0:T(128)}, f32[3,32,128]{2,1,0:T(8,128)}, f32[3,32,128]{2,1,0:T(8,128)}, f32[2,32,128]{2,1,0:T(8,128)S(1)}, /*index=5*/s32[1,64]{1,0:T(1,128)S(1)}) %tuple.37, ...), branch_computations={%region_0.1_spmd, %region_1.2_spmd} | conditional | bytes 8 | solution.py:572
  2.0 55.1 %branch_0_fun.1 = (f32[3,32,128]{2,1,0:T(8,128)S(1)}, f32[3,32,128]{2,1,0:T(8,128)S(1)}, f32[8,128]{1,0:T(8,128)S(1)}) custom-call(s32[1]{0:T(128)} %get-tuple-element.33.shift_s, f32[1]{0:T(128)} %get-tuple-element.34.strain_s, f32[3,32,128]{2,1,0:T(8,128)} %get-tuple-element.35.pos_r, f32[3,32,128]{2,1,0:T(8,128)} %get-tuple-element.36.vel_r, ...), custom_call_target="tpu_custom_call" | custom-call | tf_op jit(solution)/shard_map/cond/branch_0_fun/pallas_call | solution.py:572
  57.1 0.5 slice.7
  57.6 0.6 %copy.18 = f32[3,1,4096]{2,1,0:T(1,128)} copy(f32[3,1,4096]{2,1,0:T(1,128)S(1)} %bitcast.17) | data formatting | bytes 98304
  58.2 0.6 %copy.19 = f32[3,1,4096]{2,1,0:T(1,128)} copy(f32[3,1,4096]{2,1,0:T(1,128)S(1)} %bitcast.18) | data formatting | bytes 98304
Async XLA Ops:
  0.6 0.8 %copy-start = (f32[2,1,4096]{2,1,0:T(1,128)S(1)}, f32[2,1,4096]{2,1,0:T(1,128)}, u32[]{:S(2)}) copy-start(f32[2,1,4096]{2,1,0:T(1,128)} %param.10) | copy-start | bytes 98308
  1.3 0.7 %copy-start.1 = (s32[1,64]{1,0:T(1,128)S(1)}, s32[1,64]{1,0:T(1,128)}, u32[]{:S(2)}) copy-start(s32[1,64]{1,0:T(1,128)} %param.11) | copy-start | bytes 772

commit v5 on v4

--- a/solution.py
+++ b/solution.py
@@ -208,7 +208,7 @@
             weights[...] = same.astype(f32).astype(jnp.bfloat16)
 
         def spread_centres():
-            step = 4 if LP % 4 == 0 else 1
+            step = 8 if LP % 8 == 0 else 1
 
             def some(c, carry):
                 turned = []
@@ -327,7 +327,10 @@
                         fx = fx + mx
                         fy = fy + m * dy
                         fz = fz + m * dz
-                        virial = virial + mx * dy
+                        if not fresh:
+                            virial = virial + mx * dy
+                    if fresh:
+                        virial = virial + ey * (fx + fx)
                     facc[pl.ds(0 * TB + grp * 8, 8), wide] = fx
                     facc[pl.ds(1 * TB + grp * 8, 8), wide] = fy
                     facc[pl.ds(2 * TB + grp * 8, 8), wide] = fz

time: 59.1 us -> 58.1 us (0.983); the launches traced: 58.8 us -> 58.6 us
  no operation moved by 1% of the time
where the time goes in v5:
time: 58.1 us; the launch traced here: 58.6 us
  Pallas kernels  54.9 us (94%)
  local copies, waits for them, and re-layouts  2.41 us (4%)
  between operations  1.34 us (2%)
    pallas_call x1, Pallas kernels, per_device(): lax.switch(image_shift[0] // (2 * LP * NQ), branches, *args)  54.9 us
    unnamed x6, local copies, waits for them, and re-layouts  1.89 us

profile of v5, /device:TPU:4, one launch (start us, length us, event | category | flops | bytes accessed | tf_op | source)
XLA Modules:
  0.0 58.6 jit_solution(17323707133351398875)
XLA Ops:
  0.6 0.0 copy-start
  1.3 0.0 copy-start.1
  1.3 0.1 copy-done
  1.4 0.6 %copy-done.1 = s32[1,64]{1,0:T(1,128)S(1)} copy-done((s32[1,64]{1,0:T(1,128)S(1)}, s32[1,64]{1,0:T(1,128)}, u32[]{:S(2)}) %copy-start.1) | copy-done | bytes 280
  2.0 54.9 %conditional.1 = ((f32[3,32,128]{2,1,0:T(8,128)S(1)}, f32[3,32,128]{2,1,0:T(8,128)S(1)}, f32[8,128]{1,0:T(8,128)S(1)})) conditional(s32[]{:T(128)} %clamp.3, (s32[1]{0:T(128)}, f32[1]{0:T(128)}, f32[3,32,128]{2,1,0:T(8,128)}, f32[3,32,128]{2,1,0:T(8,128)}, f32[2,32,128]{2,1,0:T(8,128)S(1)}, /*index=5*/s32[1,64]{1,0:T(1,128)S(1)}) %tuple.37, ...), branch_computations={%region_0.1_spmd, %region_1.2_spmd} | conditional | bytes 8 | solution.py:575
  2.0 54.9 %branch_0_fun.1 = (f32[3,32,128]{2,1,0:T(8,128)S(1)}, f32[3,32,128]{2,1,0:T(8,128)S(1)}, f32[8,128]{1,0:T(8,128)S(1)}) custom-call(s32[1]{0:T(128)} %get-tuple-element.33.shift_s, f32[1]{0:T(128)} %get-tuple-element.34.strain_s, f32[3,32,128]{2,1,0:T(8,128)} %get-tuple-element.35.pos_r, f32[3,32,128]{2,1,0:T(8,128)} %get-tuple-element.36.vel_r, ...), custom_call_target="tpu_custom_call" | custom-call | tf_op jit(solution)/shard_map/cond/branch_0_fun/pallas_call | solution.py:575
  56.9 0.5 slice.7
  57.4 0.6 %copy.18 = f32[3,1,4096]{2,1,0:T(1,128)} copy(f32[3,1,4096]{2,1,0:T(1,128)S(1)} %bitcast.17) | data formatting | bytes 98304
  58.0 0.6 %copy.19 = f32[3,1,4096]{2,1,0:T(1,128)} copy(f32[3,1,4096]{2,1,0:T(1,128)S(1)} %bitcast.18) | data formatting | bytes 98304
Async XLA Ops:
  0.6 0.8 %copy-start = (f32[2,1,4096]{2,1,0:T(1,128)S(1)}, f32[2,1,4096]{2,1,0:T(1,128)}, u32[]{:S(2)}) copy-start(f32[2,1,4096]{2,1,0:T(1,128)} %param.10) | copy-start | bytes 98308
  1.3 0.7 %copy-start.1 = (s32[1,64]{1,0:T(1,128)S(1)}, s32[1,64]{1,0:T(1,128)}, u32[]{:S(2)}) copy-start(s32[1,64]{1,0:T(1,128)} %param.11) | copy-start | bytes 772
